TPU v7x, 32 devices: a whole 2x2x4 slice. The times are simulated.
32 devices in a mesh: depth: 4 (over z), imgx: 4 (over y, core), imgy: 2 (over x).
Axes of the slice: x: 2, y: 2, z: 4, core: 2. Of those that a mesh axis runs over, the one named last changes fastest.
Arguments:
- emissivity: bfloat16 [32, 512, 256], P('depth', 'imgx', 'imgy'), may hold values from 0.099609375 to 10
- bin_index: int32 [32, 512, 256], P('depth', 'imgx', 'imgy'), may hold values from 0 to 127
- color_table: bfloat16 [4, 128], replicated, may hold values from 0.049804688 to 1
- brick_order: int32 [4], replicated, may hold values from 0 to 3, each once
Outputs:
- image: float32 [4, 512, 256], P(None, 'imgx', 'imgy')
Inputs may be any that keep to these rules, and one draw needn't show every extreme that they name: brick_order names every brick index once.
All inputs are finite; a program needn't handle non-finite values.
Results may differ from a plain program's by a relative error of at most 0.0003.
Values sent between devices are 32-bit elements; how exact they have to be, the bound alone decides.
A program may use at most 64 MiB of HBM per device.

v0:
```python
import jax
import jax.numpy as jnp
from jax import lax
from jax.sharding import PartitionSpec as P


def on_device(emissivity, bin_index, color_table, brick_order):
    depth_cells, cols_x, cols_y = emissivity.shape
    pixels = cols_x * cols_y
    devices = lax.axis_size("depth")
    ray_step = 2.0 / (depth_cells * devices)
    levels = jnp.arange(color_table.shape[1], dtype=jnp.int32)

    def lookup(layer_bins):
        onehot = (layer_bins.reshape(1, pixels) == levels[:, None]).astype(jnp.bfloat16)
        return jnp.dot(color_table, onehot, preferred_element_type=jnp.float32)

    looked = lax.map(lookup, bin_index)
    bright = emissivity.reshape(depth_cells, pixels).astype(jnp.float32)
    glow_rgb = bright[:, None, :] * looked[:, 0:3, :]
    absorb_rate = bright * looked[:, 3, :]
    depth_in = jnp.cumsum(absorb_rate, axis=0) - absorb_rate
    light_in = jnp.exp(-ray_step * depth_in)
    color_sum = jnp.sum(ray_step * glow_rgb * light_in[:, None, :], axis=0)
    passed = jnp.exp(-ray_step * jnp.sum(absorb_rate, axis=0))
    piece_len = pixels // devices
    stacked = jnp.concatenate([color_sum, passed[None]], 0)[None]
    received = lax.all_to_all(stacked, "depth", split_axis=2, concat_axis=0, tiled=True)
    ordered = jnp.take(received, brick_order, axis=0)
    passed_all = ordered[:, 3, :]
    ahead_light = jnp.cumprod(
        jnp.concatenate([jnp.ones((1, piece_len), jnp.float32), passed_all[:-1]], 0), axis=0
    )
    my_color = jnp.sum(ordered[:, 0:3, :] * ahead_light[:, None, :], axis=0)
    through = jnp.prod(passed_all, axis=0)
    my_piece = jnp.concatenate([my_color, (1.0 - through)[None]], 0)
    full_tile = lax.all_gather(my_piece, "depth", axis=1, tiled=True)
    return full_tile.reshape(4, cols_x, cols_y)


def solution(mesh):
    return jax.shard_map(
        on_device,
        mesh=mesh,
        in_specs=(P("depth", "imgx", "imgy"), P("depth", "imgx", "imgy"), P(), P()),
        out_specs=P(None, "imgx", "imgy"),
        check_vma=False,
    )
```

profile of v0, /device:TPU:0, one launch (start us, length us, event | category | flops | bytes accessed | tf_op | source)
XLA Modules:
  0.0 172.7 jit_solution(10692280450666354)
XLA Ops:
  0.0 0.0 copy-start
  0.0 23.3 %while.11 = (s32[]{:T(128)}, f32[8,4,16384]{2,1,0:T(4,128)S(1)}, s32[8,128,128]{2,1,0:T(8,128)}, bf16[4,128]{1,0:T(4,128)(2,1)}, s32[]{:T(128)}) while((s32[]{:T(128)}, f32[8,4,16384]{2,1,0:T(4,128)S(1)}, s32[8,128,128]{2,1,0:T(8,128)}, bf16[4,128]{1,0:T(4,128)(2,1)}, s32[]{:T(128)}) %tuple.22), condition=%wide.region_1.2_spmd.clone, body=%wide.region_0.1_spmd.clone.sunk | while | flops 18874368 | bytes 459845 | solution.py:18
  0.0 0.9 dynamic-slice_bitcast_fusion.2
  0.9 2.1 %fusion.16 = f32[8,4,16384]{2,1,0:T(4,128)S(1)} fusion(f32[8,4,16384]{2,1,0:T(4,128)S(1)} %get-tuple-element.84, s32[]{:T(128)} %get-tuple-element.83, bf16[4,128]{1,0:T(4,128)(2,1)} %get-tuple-element.91, s32[16384]{0:T(1024)S(1)} %dynamic-slice_bitcast_fusion.2), kind=kOutput, calls=%fused_computation.3.clone.1 | convolution fusion | flops 18874368 | bytes 328708 | tf_op jit(solution)/shard_map/while/body/eval_jaxpr/dot_general | solution.py:16
  3.0 0.8 dynamic-slice_bitcast_fusion.2
  3.8 2.1 %fusion.16 = f32[8,4,16384]{2,1,0:T(4,128)S(1)} fusion(f32[8,4,16384]{2,1,0:T(4,128)S(1)} %get-tuple-element.84, s32[]{:T(128)} %get-tuple-element.83, bf16[4,128]{1,0:T(4,128)(2,1)} %get-tuple-element.91, s32[16384]{0:T(1024)S(1)} %dynamic-slice_bitcast_fusion.2), kind=kOutput, calls=%fused_computation.3.clone.1 | convolution fusion | flops 18874368 | bytes 328708 | tf_op jit(solution)/shard_map/while/body/eval_jaxpr/dot_general | solution.py:16
  5.9 0.8 dynamic-slice_bitcast_fusion.2
  6.7 2.1 %fusion.16 = f32[8,4,16384]{2,1,0:T(4,128)S(1)} fusion(f32[8,4,16384]{2,1,0:T(4,128)S(1)} %get-tuple-element.84, s32[]{:T(128)} %get-tuple-element.83, bf16[4,128]{1,0:T(4,128)(2,1)} %get-tuple-element.91, s32[16384]{0:T(1024)S(1)} %dynamic-slice_bitcast_fusion.2), kind=kOutput, calls=%fused_computation.3.clone.1 | convolution fusion | flops 18874368 | bytes 328708 | tf_op jit(solution)/shard_map/while/body/eval_jaxpr/dot_general | solution.py:16
  8.8 0.8 dynamic-slice_bitcast_fusion.2
  9.6 2.1 %fusion.16 = f32[8,4,16384]{2,1,0:T(4,128)S(1)} fusion(f32[8,4,16384]{2,1,0:T(4,128)S(1)} %get-tuple-element.84, s32[]{:T(128)} %get-tuple-element.83, bf16[4,128]{1,0:T(4,128)(2,1)} %get-tuple-element.91, s32[16384]{0:T(1024)S(1)} %dynamic-slice_bitcast_fusion.2), kind=kOutput, calls=%fused_computation.3.clone.1 | convolution fusion | flops 18874368 | bytes 328708 | tf_op jit(solution)/shard_map/while/body/eval_jaxpr/dot_general | solution.py:16
  11.7 0.8 dynamic-slice_bitcast_fusion.2
  12.5 2.1 %fusion.16 = f32[8,4,16384]{2,1,0:T(4,128)S(1)} fusion(f32[8,4,16384]{2,1,0:T(4,128)S(1)} %get-tuple-element.84, s32[]{:T(128)} %get-tuple-element.83, bf16[4,128]{1,0:T(4,128)(2,1)} %get-tuple-element.91, s32[16384]{0:T(1024)S(1)} %dynamic-slice_bitcast_fusion.2), kind=kOutput, calls=%fused_computation.3.clone.1 | convolution fusion | flops 18874368 | bytes 328708 | tf_op jit(solution)/shard_map/while/body/eval_jaxpr/dot_general | solution.py:16
  14.6 0.8 dynamic-slice_bitcast_fusion.2
  15.4 2.1 %fusion.16 = f32[8,4,16384]{2,1,0:T(4,128)S(1)} fusion(f32[8,4,16384]{2,1,0:T(4,128)S(1)} %get-tuple-element.84, s32[]{:T(128)} %get-tuple-element.83, bf16[4,128]{1,0:T(4,128)(2,1)} %get-tuple-element.91, s32[16384]{0:T(1024)S(1)} %dynamic-slice_bitcast_fusion.2), kind=kOutput, calls=%fused_computation.3.clone.1 | convolution fusion | flops 18874368 | bytes 328708 | tf_op jit(solution)/shard_map/while/body/eval_jaxpr/dot_general | solution.py:16
  17.5 0.8 dynamic-slice_bitcast_fusion.2
  18.3 2.1 %fusion.16 = f32[8,4,16384]{2,1,0:T(4,128)S(1)} fusion(f32[8,4,16384]{2,1,0:T(4,128)S(1)} %get-tuple-element.84, s32[]{:T(128)} %get-tuple-element.83, bf16[4,128]{1,0:T(4,128)(2,1)} %get-tuple-element.91, s32[16384]{0:T(1024)S(1)} %dynamic-slice_bitcast_fusion.2), kind=kOutput, calls=%fused_computation.3.clone.1 | convolution fusion | flops 18874368 | bytes 328708 | tf_op jit(solution)/shard_map/while/body/eval_jaxpr/dot_general | solution.py:16
  20.4 0.8 dynamic-slice_bitcast_fusion.2
  21.2 2.1 %fusion.16 = f32[8,4,16384]{2,1,0:T(4,128)S(1)} fusion(f32[8,4,16384]{2,1,0:T(4,128)S(1)} %get-tuple-element.84, s32[]{:T(128)} %get-tuple-element.83, bf16[4,128]{1,0:T(4,128)(2,1)} %get-tuple-element.91, s32[16384]{0:T(1024)S(1)} %dynamic-slice_bitcast_fusion.2), kind=kOutput, calls=%fused_computation.3.clone.1 | convolution fusion | flops 18874368 | bytes 328708 | tf_op jit(solution)/shard_map/while/body/eval_jaxpr/dot_general | solution.py:16
  23.3 0.0 copy-done
  23.3 0.1 fusion.11
  23.4 0.5 slice.18
  23.9 1.2 fusion.6
  25.2 0.3 copy.26
  25.5 0.3 copy.25
  25.8 0.7 fusion.7
  26.6 0.9 multiply_reduce_fusion
  27.5 0.1 pad_maximum_fusion
  27.6 5.1 %copy.8 = f32[4,16384]{0,1:T(8,128)} copy(f32[4,16384]{1,0:T(4,128)S(1)} %pad_maximum_fusion) | data formatting | bytes 524288 | tf_op jit(solution)/shard_map/concatenate | solution.py:27
  32.7 0.5 broadcast.39
  33.2 74.4 %reduce.1 = f32[16384,4]{1,0:T(8,128)} reduce(f32[16384,1,4]{2,1,0:T(1,128)} %bitcast.46, f32[]{:T(128)} %broadcast.39), dimensions={1}, to_apply=%bitcast.33.reduce_sub_computation | reduce | bytes 524292
  107.6 0.0 copy-start.1
  107.6 9.1 %reshape.72 = f32[4,1,16384]{2,1,0:T(1,128)} reshape(f32[16384,4]{1,0:T(8,128)} %reduce.1) | data formatting | bytes 524288
  116.7 6.3 %all-to-all-start = ((f32[4,1,16384]{2,1,0:T(1,128)}), f32[4,1,16384]{2,1,0:T(1,128)S(1)}, u32[]{:S(2)}, u32[]{:S(2)}) async-start(f32[4,1,16384]{2,1,0:T(1,128)} %reshape.72), calls=%async_computation | async-start | bytes 524288 | tf_op jit(solution)/shard_map/all_to_all | solution.py:28
  123.0 0.0 copy-done.1
  123.0 8.9 %all-to-all-done = f32[4,1,16384]{2,1,0:T(1,128)S(1)} async-done(((f32[4,1,16384]{2,1,0:T(1,128)}), f32[4,1,16384]{2,1,0:T(1,128)S(1)}, u32[]{:S(2)}, u32[]{:S(2)}) %all-to-all-start) | async-done | bytes 262176 | tf_op jit(solution)/shard_map/all_to_all | solution.py:28
  131.9 1.3 reduce.2
  133.2 17.7 %reshape.73 = f32[16384,1,4]{2,1,0:T(1,128)} reshape(f32[4,16384]{1,0:T(4,128)S(1)} %reduce.2) | data formatting | bytes 524288
  150.9 5.3 %copy.10 = f32[1,4,4,4096]{3,1,2,0:T(4,128)S(1)} copy(f32[1,4,4,4096]{1,3,2,0:T(8,128)} %bitcast.47) | data formatting | bytes 524288 | tf_op jit(solution)/shard_map/all_to_all | solution.py:28
  156.2 0.7 gather_fusion
  156.9 0.1 broadcast_select_fusion
  157.0 0.1 slice.25
  157.1 0.1 slice_reduce_fusion
  157.2 0.1 reduce_window.12
  157.3 0.1 fusion.9
  157.5 14.5 %all_gather.3 = f32[4,16384]{1,0:T(4,128)S(1)} all-gather(f32[4,4096]{1,0:T(4,128)S(1)} %pad_maximum_fusion.1), channel_id=1, replica_groups=mesh['depth'=4,'imgx'=4,'imgy'=2] {'depth'}, dimensions={1}, use_global_device_ids=true | all-gather | bytes 327680 | tf_op jit(solution)/shard_map/all_gather | solution.py:37
  171.9 0.7 copy.27
  (8 shorter events, 0.1 us)
Async XLA Ops:
  0.0 23.3 %copy-start = (bf16[8,128,128]{2,1,0:T(8,128)(2,1)S(1)}, bf16[8,128,128]{2,1,0:T(8,128)(2,1)}, u32[]{:S(2)}) copy-start(bf16[8,128,128]{2,1,0:T(8,128)(2,1)} %param.6) | copy-start | bytes 786436
  107.6 15.4 %copy-start.1 = (s32[4]{0:T(128)S(1)}, s32[4]{0:T(128)}, u32[]{:S(2)}) copy-start(s32[4]{0:T(128)} %param.9) | copy-start | bytes 52
  116.7 15.3 %all-to-all-start = ((f32[4,1,16384]{2,1,0:T(1,128)}), f32[4,1,16384]{2,1,0:T(1,128)S(1)}, u32[]{:S(2)}, u32[]{:S(2)}) async-start(f32[4,1,16384]{2,1,0:T(1,128)} %reshape.72), calls=%async_computation | async-start | bytes 524288 | tf_op jit(solution)/shard_map/all_to_all | solution.py:28
where the time goes:
time: 173 us
  other arithmetic  79.2 us (46%)
  local copies, waits for them, and re-layouts  47.1 us (27%)
  matrix products  16.5 us (10%)
  blocking collectives  14.5 us (8%)
  waiting for transfers between devices  8.87 us (5%)
  starting transfers between devices  6.35 us (4%)
    unnamed x1, other arithmetic  74.4 us
    unnamed x11, local copies, waits for them, and re-layouts  28.7 us
    dot_general x8, matrix products, lookup(): return jnp.dot(color_table, onehot, preferred_element_type=jnp.float32)  16.5 us
    all_gather x1, blocking collectives, on_device(): full_tile = lax.all_gather(my_piece, 'depth', axis=1, tiled=True)  14.5 us
    all_to_all x1, waiting for transfers between devices, on_device(): lax.all_to_all(stacked, 'depth', split_axis=2, concat_axis=0, tiled=True)  8.87 us
    eq x8, local copies, waits for them, and re-layouts, lookup(): layer_bins.reshape(1, pixels) == levels[:, None]  6.79 us
    all_to_all x1, starting transfers between devices, on_device(): lax.all_to_all(stacked, 'depth', split_axis=2, concat_axis=0, tiled=True)  6.35 us
    all_to_all x1, local copies, waits for them, and re-layouts, on_device(): lax.all_to_all(stacked, 'depth', split_axis=2, concat_axis=0, tiled=True)  5.3 us
  transfers between devices with their start and end apart: 1, of which 1 were waited for; matrix products, arithmetic and copies ran while one was open for 0% of the time, Pallas kernels for 0%

commit v1 on v0

--- a/solution.py
+++ b/solution.py
@@ -25,7 +25,9 @@
     passed = jnp.exp(-ray_step * jnp.sum(absorb_rate, axis=0))
     piece_len = pixels // devices
     stacked = jnp.concatenate([color_sum, passed[None]], 0)[None]
-    received = lax.all_to_all(stacked, "depth", split_axis=2, concat_axis=0, tiled=True)
+    pieces = jnp.split(stacked, lax.axis_size("depth"), axis=2)
+    incoming = lax.all_to_all(jnp.stack(pieces), "depth", 0, 0)
+    received = jnp.concatenate(incoming, axis=0)
     ordered = jnp.take(received, brick_order, axis=0)
     passed_all = ordered[:, 3, :]
     ahead_light = jnp.cumprod(

time: 173 us -> 60.8 us (0.35)
  other arithmetic: 79.2 us -> 4.31 us
  local copies, waits for them, and re-layouts: 47.1 us -> 9.49 us
    unnamed x1 -> x0, other arithmetic: 74.4 us -> none
    unnamed x11 -> x8, local copies, waits for them, and re-layouts: 28.7 us -> 1.39 us
    all_to_all x1 -> x0, local copies, waits for them, and re-layouts: 5.3 us -> none  [on_device(): lax.all_to_all(stacked, 'depth', split_axis=2, concat_axis=0, tiled=True)]
    concatenate x1 -> x0, local copies, waits for them, and re-layouts: 5.08 us -> none  [on_device(): stacked = jnp.concatenate([color_sum, passed[None]], 0)[None]]
where the time goes in v1:
time: 60.8 us; the launch traced here: 60.1 us
  matrix products  16.5 us (27%)
  blocking collectives  14.5 us (24%)
  local copies, waits for them, and re-layouts  9.49 us (16%)
  waiting for transfers between devices  8.87 us (15%)
  starting transfers between devices  6.35 us (10%)
  other arithmetic  4.31 us (7%)
    dot_general x8, matrix products, lookup(): return jnp.dot(color_table, onehot, preferred_element_type=jnp.float32)  16.5 us
    all_gather x1, blocking collectives, on_device(): full_tile = lax.all_gather(my_piece, 'depth', axis=1, tiled=True)  14.5 us
    all_to_all x1, waiting for transfers between devices, on_device(): incoming = lax.all_to_all(jnp.stack(pieces), 'depth', 0, 0)  8.87 us
    eq x8, local copies, waits for them, and re-layouts, lookup(): layer_bins.reshape(1, pixels) == levels[:, None]  6.79 us
    all_to_all x1, starting transfers between devices, on_device(): incoming = lax.all_to_all(jnp.stack(pieces), 'depth', 0, 0)  6.35 us
    unnamed x8, local copies, waits for them, and re-layouts  1.39 us
    another operation x1, other arithmetic, on_device(): depth_in = jnp.cumsum(absorb_rate, axis=0) - absorb_rate  1.24 us
  transfers between devices with their start and end apart: 1, of which 1 were waited for; matrix products, arithmetic and copies ran while one was open for 0% of the time, Pallas kernels for 0%

profile of v1, /device:TPU:0, one launch (start us, length us, event | category | flops | bytes accessed | tf_op | source)
XLA Modules:
  0.0 60.1 jit_solution(4742558048029132267)
XLA Ops:
  0.0 0.0 copy-start
  0.0 23.3 %while.11 = (s32[]{:T(128)}, f32[8,4,16384]{2,1,0:T(4,128)S(1)}, s32[8,128,128]{2,1,0:T(8,128)}, bf16[4,128]{1,0:T(4,128)(2,1)}, s32[]{:T(128)}) while((s32[]{:T(128)}, f32[8,4,16384]{2,1,0:T(4,128)S(1)}, s32[8,128,128]{2,1,0:T(8,128)}, bf16[4,128]{1,0:T(4,128)(2,1)}, s32[]{:T(128)}) %tuple.25), condition=%wide.region_1.2_spmd.clone, body=%wide.region_0.1_spmd.clone.sunk | while | flops 18874368 | bytes 459845 | solution.py:18
  0.0 0.9 %dynamic-slice_bitcast_fusion.2 = s32[16384]{0:T(1024)S(1)} fusion(s32[8,128,128]{2,1,0:T(8,128)} %get-tuple-element.94, s32[]{:T(128)} %get-tuple-element.87), kind=kLoop, calls=%fused_computation.6.clone.1 | loop fusion | bytes 131076 | tf_op jit(solution)/shard_map/while/body/eval_jaxpr/eq | solution.py:15
  0.9 2.1 %fusion.16 = f32[8,4,16384]{2,1,0:T(4,128)S(1)} fusion(f32[8,4,16384]{2,1,0:T(4,128)S(1)} %get-tuple-element.88, s32[]{:T(128)} %get-tuple-element.87, bf16[4,128]{1,0:T(4,128)(2,1)} %get-tuple-element.95, s32[16384]{0:T(1024)S(1)} %dynamic-slice_bitcast_fusion.2), kind=kOutput, calls=%fused_computation.3.clone.1 | convolution fusion | flops 18874368 | bytes 328708 | tf_op jit(solution)/shard_map/while/body/eval_jaxpr/dot_general | solution.py:16
  3.0 0.8 %dynamic-slice_bitcast_fusion.2 = s32[16384]{0:T(1024)S(1)} fusion(s32[8,128,128]{2,1,0:T(8,128)} %get-tuple-element.94, s32[]{:T(128)} %get-tuple-element.87), kind=kLoop, calls=%fused_computation.6.clone.1 | loop fusion | bytes 131076 | tf_op jit(solution)/shard_map/while/body/eval_jaxpr/eq | solution.py:15
  3.8 2.1 %fusion.16 = f32[8,4,16384]{2,1,0:T(4,128)S(1)} fusion(f32[8,4,16384]{2,1,0:T(4,128)S(1)} %get-tuple-element.88, s32[]{:T(128)} %get-tuple-element.87, bf16[4,128]{1,0:T(4,128)(2,1)} %get-tuple-element.95, s32[16384]{0:T(1024)S(1)} %dynamic-slice_bitcast_fusion.2), kind=kOutput, calls=%fused_computation.3.clone.1 | convolution fusion | flops 18874368 | bytes 328708 | tf_op jit(solution)/shard_map/while/body/eval_jaxpr/dot_general | solution.py:16
  5.9 0.8 %dynamic-slice_bitcast_fusion.2 = s32[16384]{0:T(1024)S(1)} fusion(s32[8,128,128]{2,1,0:T(8,128)} %get-tuple-element.94, s32[]{:T(128)} %get-tuple-element.87), kind=kLoop, calls=%fused_computation.6.clone.1 | loop fusion | bytes 131076 | tf_op jit(solution)/shard_map/while/body/eval_jaxpr/eq | solution.py:15
  6.7 2.1 %fusion.16 = f32[8,4,16384]{2,1,0:T(4,128)S(1)} fusion(f32[8,4,16384]{2,1,0:T(4,128)S(1)} %get-tuple-element.88, s32[]{:T(128)} %get-tuple-element.87, bf16[4,128]{1,0:T(4,128)(2,1)} %get-tuple-element.95, s32[16384]{0:T(1024)S(1)} %dynamic-slice_bitcast_fusion.2), kind=kOutput, calls=%fused_computation.3.clone.1 | convolution fusion | flops 18874368 | bytes 328708 | tf_op jit(solution)/shard_map/while/body/eval_jaxpr/dot_general | solution.py:16
  8.8 0.8 %dynamic-slice_bitcast_fusion.2 = s32[16384]{0:T(1024)S(1)} fusion(s32[8,128,128]{2,1,0:T(8,128)} %get-tuple-element.94, s32[]{:T(128)} %get-tuple-element.87), kind=kLoop, calls=%fused_computation.6.clone.1 | loop fusion | bytes 131076 | tf_op jit(solution)/shard_map/while/body/eval_jaxpr/eq | solution.py:15
  9.6 2.1 %fusion.16 = f32[8,4,16384]{2,1,0:T(4,128)S(1)} fusion(f32[8,4,16384]{2,1,0:T(4,128)S(1)} %get-tuple-element.88, s32[]{:T(128)} %get-tuple-element.87, bf16[4,128]{1,0:T(4,128)(2,1)} %get-tuple-element.95, s32[16384]{0:T(1024)S(1)} %dynamic-slice_bitcast_fusion.2), kind=kOutput, calls=%fused_computation.3.clone.1 | convolution fusion | flops 18874368 | bytes 328708 | tf_op jit(solution)/shard_map/while/body/eval_jaxpr/dot_general | solution.py:16
  11.7 0.8 %dynamic-slice_bitcast_fusion.2 = s32[16384]{0:T(1024)S(1)} fusion(s32[8,128,128]{2,1,0:T(8,128)} %get-tuple-element.94, s32[]{:T(128)} %get-tuple-element.87), kind=kLoop, calls=%fused_computation.6.clone.1 | loop fusion | bytes 131076 | tf_op jit(solution)/shard_map/while/body/eval_jaxpr/eq | solution.py:15
  12.5 2.1 %fusion.16 = f32[8,4,16384]{2,1,0:T(4,128)S(1)} fusion(f32[8,4,16384]{2,1,0:T(4,128)S(1)} %get-tuple-element.88, s32[]{:T(128)} %get-tuple-element.87, bf16[4,128]{1,0:T(4,128)(2,1)} %get-tuple-element.95, s32[16384]{0:T(1024)S(1)} %dynamic-slice_bitcast_fusion.2), kind=kOutput, calls=%fused_computation.3.clone.1 | convolution fusion | flops 18874368 | bytes 328708 | tf_op jit(solution)/shard_map/while/body/eval_jaxpr/dot_general | solution.py:16
  14.6 0.8 %dynamic-slice_bitcast_fusion.2 = s32[16384]{0:T(1024)S(1)} fusion(s32[8,128,128]{2,1,0:T(8,128)} %get-tuple-element.94, s32[]{:T(128)} %get-tuple-element.87), kind=kLoop, calls=%fused_computation.6.clone.1 | loop fusion | bytes 131076 | tf_op jit(solution)/shard_map/while/body/eval_jaxpr/eq | solution.py:15
  15.4 2.1 %fusion.16 = f32[8,4,16384]{2,1,0:T(4,128)S(1)} fusion(f32[8,4,16384]{2,1,0:T(4,128)S(1)} %get-tuple-element.88, s32[]{:T(128)} %get-tuple-element.87, bf16[4,128]{1,0:T(4,128)(2,1)} %get-tuple-element.95, s32[16384]{0:T(1024)S(1)} %dynamic-slice_bitcast_fusion.2), kind=kOutput, calls=%fused_computation.3.clone.1 | convolution fusion | flops 18874368 | bytes 328708 | tf_op jit(solution)/shard_map/while/body/eval_jaxpr/dot_general | solution.py:16
  17.5 0.8 %dynamic-slice_bitcast_fusion.2 = s32[16384]{0:T(1024)S(1)} fusion(s32[8,128,128]{2,1,0:T(8,128)} %get-tuple-element.94, s32[]{:T(128)} %get-tuple-element.87), kind=kLoop, calls=%fused_computation.6.clone.1 | loop fusion | bytes 131076 | tf_op jit(solution)/shard_map/while/body/eval_jaxpr/eq | solution.py:15
  18.3 2.1 %fusion.16 = f32[8,4,16384]{2,1,0:T(4,128)S(1)} fusion(f32[8,4,16384]{2,1,0:T(4,128)S(1)} %get-tuple-element.88, s32[]{:T(128)} %get-tuple-element.87, bf16[4,128]{1,0:T(4,128)(2,1)} %get-tuple-element.95, s32[16384]{0:T(1024)S(1)} %dynamic-slice_bitcast_fusion.2), kind=kOutput, calls=%fused_computation.3.clone.1 | convolution fusion | flops 18874368 | bytes 328708 | tf_op jit(solution)/shard_map/while/body/eval_jaxpr/dot_general | solution.py:16
  20.4 0.8 %dynamic-slice_bitcast_fusion.2 = s32[16384]{0:T(1024)S(1)} fusion(s32[8,128,128]{2,1,0:T(8,128)} %get-tuple-element.94, s32[]{:T(128)} %get-tuple-element.87), kind=kLoop, calls=%fused_computation.6.clone.1 | loop fusion | bytes 131076 | tf_op jit(solution)/shard_map/while/body/eval_jaxpr/eq | solution.py:15
  21.2 2.1 %fusion.16 = f32[8,4,16384]{2,1,0:T(4,128)S(1)} fusion(f32[8,4,16384]{2,1,0:T(4,128)S(1)} %get-tuple-element.88, s32[]{:T(128)} %get-tuple-element.87, bf16[4,128]{1,0:T(4,128)(2,1)} %get-tuple-element.95, s32[16384]{0:T(1024)S(1)} %dynamic-slice_bitcast_fusion.2), kind=kOutput, calls=%fused_computation.3.clone.1 | convolution fusion | flops 18874368 | bytes 328708 | tf_op jit(solution)/shard_map/while/body/eval_jaxpr/dot_general | solution.py:16
  23.3 0.0 copy-done
  23.3 0.1 fusion.11
  23.4 0.5 slice.18
  23.9 1.2 %fusion.6 = f32[8,1,16384]{2,1,0:T(1,128)S(1)} fusion(f32[8,1,16384]{2,1,0:T(1,128)S(1)} %bitcast.50, f32[8,4,16384]{2,1,0:T(4,128)S(1)} %get-tuple-element.32), kind=kOutput, calls=%fused_computation.10 | output fusion | flops 1441792 | bytes 1572864 | tf_op jit(solution)/shard_map/jit(cumsum)/reduce_window_sum | solution.py:22
  25.2 0.3 copy.27
  25.5 0.3 copy.26
  25.8 0.7 %fusion.7 = f32[16384]{0:T(1024)S(1)} fusion(f32[8,1,16384]{2,1,0:T(1,128)S(1)} %slice.18, f32[1,8,128,128]{3,2,1,0:T(8,128)S(1)} %get-tuple-element.56), kind=kLoop, calls=%fused_computation.14 | loop fusion | flops 245760 | bytes 1114112 | tf_op jit(solution)/shard_map/reduce_sum | solution.py:25
  26.6 0.0 copy-start.1
  26.6 0.9 %multiply_reduce_fusion = f32[3,16384]{1,0:T(4,128)S(1)} fusion(f32[8,4,16384]{2,1,0:T(4,128)S(1)} %get-tuple-element.32, f32[8,16384]{1,0:T(8,128)S(1)} %bitcast.51, f32[8,16384]{1,0:T(8,128)S(1)} %bitcast.52), kind=kLoop, calls=%fused_computation.11 | loop fusion | flops 1130496 | bytes 2818048 | tf_op jit(solution)/shard_map/reduce_sum | solution.py:24
  27.5 0.1 maximum_bitcast_fusion
  27.6 0.8 %pad_maximum_fusion = f32[4,1,4,4096]{3,2,1,0:T(4,128)} fusion(f32[1,1,4,4096]{3,2,1,0:T(4,128)S(1)} %get-tuple-element.52, f32[1,1,4,4096]{3,2,1,0:T(4,128)S(1)} %get-tuple-element.53, f32[1,1,4,4096]{3,2,1,0:T(4,128)S(1)} %get-tuple-element.54, f32[1,1,4,4096]{3,2,1,0:T(4,128)S(1)} %get-tuple-element.51), kind=kLoop, calls=%fused_computation.21 | loop fusion | flops 196608 | bytes 524288 | tf_op jit(solution)/shard_map/stack | solution.py:29
  28.4 6.3 %all-to-all-start = ((f32[4,1,4,4096]{3,2,1,0:T(4,128)}), f32[4,1,4,4096]{3,2,1,0:T(4,128)S(1)}, u32[]{:S(2)}, u32[]{:S(2)}) async-start(f32[4,1,4,4096]{3,2,1,0:T(4,128)} %pad_maximum_fusion), calls=%async_computation | async-start | bytes 524288 | tf_op jit(solution)/shard_map/all_to_all | solution.py:29
  34.8 0.0 copy-done.1
  34.8 8.9 %all-to-all-done = f32[4,1,4,4096]{3,2,1,0:T(4,128)S(1)} async-done(((f32[4,1,4,4096]{3,2,1,0:T(4,128)}), f32[4,1,4,4096]{3,2,1,0:T(4,128)S(1)}, u32[]{:S(2)}, u32[]{:S(2)}) %all-to-all-start) | async-done | bytes 262176 | tf_op jit(solution)/shard_map/all_to_all | solution.py:29
  43.7 0.7 %gather_fusion = f32[4,4,4096]{2,1,0:T(4,128)S(1)} fusion(f32[4,4,4096]{2,1,0:T(4,128)S(1)} %bitcast.53, s32[1024]{0:T(1024)S(1)} %pad_clamp_fusion), kind=kCustom, calls=%fused_computation | custom fusion | bytes 524304 | tf_op jit(solution)/shard_map/jit(_take)/gather | solution.py:31
  44.4 0.1 broadcast_select_fusion
  44.5 0.1 slice.25
  44.6 0.1 slice_reduce_fusion
  44.7 0.1 reduce_window.12
  44.8 0.1 fusion.9
  44.9 14.5 %all_gather.3 = f32[4,16384]{1,0:T(4,128)S(1)} all-gather(f32[4,4096]{1,0:T(4,128)S(1)} %pad_maximum_fusion.1), channel_id=1, replica_groups=mesh['depth'=4,'imgx'=4,'imgy'=2] {'depth'}, dimensions={1}, use_global_device_ids=true | all-gather | bytes 327680 | tf_op jit(solution)/shard_map/all_gather | solution.py:39
  59.4 0.7 %copy.28 = f32[1,4,128,128]{3,2,1,0:T(8,128)} copy(f32[1,4,128,128]{3,1,2,0:T(4,128)S(1)} %bitcast.54) | data formatting | bytes 524288
  (9 shorter events, 0.1 us)
Async XLA Ops:
  0.0 23.3 %copy-start = (bf16[8,128,128]{2,1,0:T(8,128)(2,1)S(1)}, bf16[8,128,128]{2,1,0:T(8,128)(2,1)}, u32[]{:S(2)}) copy-start(bf16[8,128,128]{2,1,0:T(8,128)(2,1)} %param.6) | copy-start | bytes 786436
  26.6 8.2 %copy-start.1 = (s32[4]{0:T(128)S(1)}, s32[4]{0:T(128)}, u32[]{:S(2)}) copy-start(s32[4]{0:T(128)} %param.9) | copy-start | bytes 52
  28.4 15.3 %all-to-all-start = ((f32[4,1,4,4096]{3,2,1,0:T(4,128)}), f32[4,1,4,4096]{3,2,1,0:T(4,128)S(1)}, u32[]{:S(2)}, u32[]{:S(2)}) async-start(f32[4,1,4,4096]{3,2,1,0:T(4,128)} %pad_maximum_fusion), calls=%async_computation | async-start | bytes 524288 | tf_op jit(solution)/shard_map/all_to_all | solution.py:29
